TPU v7x, 256 devices: a whole 4x4x8 slice. The times are simulated.
256 devices in a mesh: af: 4 (over y), sa: 64 (over z, x, core).
Axes of the slice: x: 4, y: 4, z: 8, core: 2. Of those that a mesh axis runs over, the one named last changes fastest.
Arguments:
- data_real: bfloat16 [64, 512, 512], P('af', 'sa'), may hold values from -0.5 to 0.5
- data_imaginary: bfloat16 [64, 512, 512], P('af', 'sa'), may hold values from -0.5 to 0.5
- wavelet_real: float32 [64], P('af'), may hold values from -2.5 to 2.5
- wavelet_imaginary: float32 [64], P('af'), may hold values from -2.5 to 2.5
- primaries_real: float32 [64, 512, 512], P('af', 'sa'), may hold values from -3 to 3
- primaries_imaginary: float32 [64, 512, 512], P('af', 'sa'), may hold values from -3 to 3
Outputs:
- updated_real: float32 [64, 512, 512], P('af', 'sa')
- updated_imaginary: float32 [64, 512, 512], P('af', 'sa')
- misfit: float32 [2], replicated
All inputs are finite; a program needn't handle non-finite values.
Results may differ from a plain program's by a relative error of at most 0.0018.
Values may be sent and summed in bfloat16 or wider, within the bound.
A program may use at most 64 MiB of HBM per device.

v0:
```python
import math
import jax
import jax.numpy as jnp
from jax import lax
from jax.sharding import Mesh
from jax.sharding import PartitionSpec as P

N = 512
F = 64
ITERS = 2
SA = ("sa_0", "sa_1", "sa_2")
AF_SA = ("af", "sa_0", "sa_1", "sa_2")
STEP_LENGTH = 0.02
THRESHOLD = 0.25


def side_by_side(arrays, axis, dim, along):
    both = jnp.concatenate(arrays, axis=along)
    result, at, finished = (lax.all_gather(both, axis, axis=dim, tiled=True), 0, [])
    for a in arrays:
        finished.append(lax.slice_in_dim(result, at, at + a.shape[along], axis=along))
        at += a.shape[along]
    return tuple(finished)


def in_one_piece(arrays, axis, split_dim, concat_dim, along):
    widths = [a.shape[along] for a in arrays]
    both = jnp.concatenate(arrays, axis=along)
    result = lax.all_to_all(both, axis, split_axis=split_dim, concat_axis=concat_dim, tiled=True)
    return tuple(jnp.split(result, [sum(widths[:k]) for k in range(1, len(widths))], axis=along))


def by_axis(value, axes):
    for axis in axes:
        value = lax.psum(value, axis)
    return value


def fourier_tables(row_index, col_index):
    phase = row_index[:, None] * col_index[None, :] % F
    angle = phase.astype(jnp.float32) * (2.0 * math.pi / F)
    factor = 1.0 / math.sqrt(F)
    return (jnp.cos(angle) * factor, jnp.sin(angle) * factor)


def highest(left, right):
    return jnp.dot(left, right, precision=lax.Precision.HIGHEST, preferred_element_type=jnp.float32)


def stacked(part_real, part_imaginary):
    return jnp.concatenate(
        [part_real.astype(jnp.bfloat16), part_imaginary.astype(jnp.bfloat16)], axis=1
    )


def shrink(values):
    return values - jnp.clip(values, -THRESHOLD, THRESHOLD)


def on_device(
    data_real, data_imaginary, wavelet_real, wavelet_imaginary, primaries_real, primaries_imaginary
):
    row_count = data_real.shape[1]
    wave_real = wavelet_real[:, None, None]
    wave_imaginary = wavelet_imaginary[:, None, None]
    current_real = primaries_real
    current_imaginary = primaries_imaginary
    own_real = data_real.astype(jnp.float32)
    own_imaginary = data_imaginary.astype(jnp.float32)
    whole_real, whole_imaginary = side_by_side((data_real, data_imaginary), SA, 1, 0)
    local_sums = []
    for iteration in range(ITERS):
        left_rows = stacked(current_real, current_imaginary)
        product_real = jnp.einsum(
            "frk,fkc->frc", left_rows, whole_real, preferred_element_type=jnp.float32
        )
        product_imaginary = jnp.einsum(
            "frk,fkc->frc", left_rows, whole_imaginary, preferred_element_type=jnp.float32
        )
        forward_real = product_real[:, :row_count] - product_imaginary[:, row_count:]
        forward_imaginary = product_imaginary[:, :row_count] + product_real[:, row_count:]
        error_real = (
            own_real
            + forward_real
            - (wave_real * current_real - wave_imaginary * current_imaginary)
        )
        error_imaginary = (
            own_imaginary
            + forward_imaginary
            - (wave_real * current_imaginary + wave_imaginary * current_real)
        )
        local_sum = jnp.sum(error_real * error_real) + jnp.sum(error_imaginary * error_imaginary)
        local_sums.append(local_sum)
        error_rows = stacked(error_real, error_imaginary)
        with_real = jnp.einsum(
            "frk,fjk->frj", error_rows, whole_real, preferred_element_type=jnp.float32
        )
        with_imaginary = jnp.einsum(
            "frk,fjk->frj", error_rows, whole_imaginary, preferred_element_type=jnp.float32
        )
        back_real = with_real[:, :row_count] + with_imaginary[:, row_count:]
        back_imaginary = with_real[:, row_count:] - with_imaginary[:, :row_count]
        gradient_real = wave_real * error_real + wave_imaginary * error_imaginary - back_real
        gradient_imaginary = (
            wave_real * error_imaginary - wave_imaginary * error_real - back_imaginary
        )
        stepped_real = current_real + STEP_LENGTH * gradient_real
        stepped_imaginary = current_imaginary + STEP_LENGTH * gradient_imaginary
        trace_real, trace_imaginary = (
            lax.all_to_all(stepped_real, "af", split_axis=2, concat_axis=0, tiled=True),
            lax.all_to_all(stepped_imaginary, "af", split_axis=2, concat_axis=0, tiled=True),
        )
        block_shape = trace_real.shape
        flat_real = trace_real.reshape(F, -1)
        flat_imaginary = trace_imaginary.reshape(F, -1)
        every_index = jnp.arange(F, dtype=jnp.int32)
        cosine, sine = fourier_tables(every_index, every_index)
        time_real = highest(cosine, flat_real) - highest(sine, flat_imaginary)
        time_imaginary = highest(sine, flat_real) + highest(cosine, flat_imaginary)
        shrunk_real = shrink(time_real)
        shrunk_imaginary = shrink(time_imaginary)
        freq_real = (highest(cosine, shrunk_real) + highest(sine, shrunk_imaginary)).reshape(
            block_shape
        )
        freq_imaginary = (highest(cosine, shrunk_imaginary) - highest(sine, shrunk_real)).reshape(
            block_shape
        )
        current_real, current_imaginary = in_one_piece((freq_real, freq_imaginary), "af", 0, 2, 1)
    totals = by_axis(jnp.stack(local_sums), AF_SA)
    misfit = totals / (F * N * N)
    return (current_real, current_imaginary, misfit)


def solution(mesh):
    split = Mesh(mesh.devices.reshape(mesh.shape["af"], 8, 4, 2), ("af", "sa_0", "sa_1", "sa_2"))
    in_specs = (
        P("af", SA, None),
        P("af", SA, None),
        P("af"),
        P("af"),
        P("af", SA, None),
        P("af", SA, None),
    )
    out_specs = (P("af", SA, None), P("af", SA, None), P())
    return jax.shard_map(
        on_device, mesh=split, in_specs=in_specs, out_specs=out_specs, check_vma=False
    )
```

profile of v0, /device:TPU:1, one launch (start us, length us, event | category | flops | bytes accessed | tf_op | source)
XLA Modules:
  0.0 275.2 jit_solution(14884716040026939522)
XLA Ops:
  7.2 1.7 pad_maximum_fusion.3
  8.9 1.0 convert_element_type.66
  9.9 1.0 convert_element_type.67
  11.0 110.2 %all-gather.2.cloned.1.call-done = bf16[32,512,512]{2,1,0:T(8,128)(2,1)} async-done(((bf16[32,8,512]{2,1,0:T(8,128)(2,1)}), bf16[32,512,512]{2,1,0:T(8,128)(2,1)}) %all-gather.2.cloned.1.call-update) | async-done | bytes 16777232 | tf_op jit(solution)/shard_map/all_gather | solution.py:19
  121.1 4.7 %fusion.6 = f32[16,16,512]{2,1,0:T(8,128)S(1)} fusion(bf16[32,512,512]{2,1,0:T(8,128)(2,1)} %all-gather.2.cloned.1.call-done, bf16[16,8,512]{2,1,0:T(8,128)(2,1)S(1)} %convert_element_type.67, bf16[16,8,512]{2,1,0:T(8,128)(2,1)S(1)} %convert_element_type.66), kind=kOutput, calls=%fused_computation.6 | convolution fusion | flops 134742016 | bytes 9175040 | tf_op jit(solution)/shard_map/frk,fkc->frc/dot_general | solution.py:77
  125.9 5.3 %fusion.14 = f32[16,16,512]{2,1,0:T(8,128)S(1)} fusion(bf16[32,512,512]{2,1,0:T(8,128)(2,1)} %all-gather.2.cloned.1.call-done, bf16[16,8,512]{2,1,0:T(8,128)(2,1)S(1)} %convert_element_type.67, bf16[16,8,512]{2,1,0:T(8,128)(2,1)S(1)} %convert_element_type.66), kind=kOutput, calls=%fused_computation.14 | convolution fusion | flops 134742016 | bytes 9175040 | tf_op jit(solution)/shard_map/frk,fkc->frc/dot_general | solution.py:74
  131.2 0.8 multiply_reduce_fusion.3
  132.1 2.3 fusion.4
  134.4 2.3 fusion.12
  136.9 0.8 copy.26
  137.8 1.5 reshape.44
  139.2 4.0 %all-to-all-start = ((f32[4,1,16384]{2,1,0:T(1,128)}), f32[4,1,16384]{2,1,0:T(1,128)S(1)}, u32[]{:S(2)}, u32[]{:S(2)}) async-start(f32[4,1,16384]{2,1,0:T(1,128)} %reshape.44), calls=%async_computation | async-start | bytes 524288 | tf_op jit(solution)/shard_map/all_to_all | solution.py:110
  143.2 0.8 copy.28
  144.0 1.5 reshape.46
  145.5 3.6 %all-to-all-done = f32[4,1,16384]{2,1,0:T(1,128)S(1)} async-done(((f32[4,1,16384]{2,1,0:T(1,128)}), f32[4,1,16384]{2,1,0:T(1,128)S(1)}, u32[]{:S(2)}, u32[]{:S(2)}) %all-to-all-start) | async-done | bytes 262176 | tf_op jit(solution)/shard_map/all_to_all | solution.py:110
  149.1 3.6 %all-to-all-start.1 = ((f32[4,1,16384]{2,1,0:T(1,128)}), f32[4,1,16384]{2,1,0:T(1,128)S(1)}, u32[]{:S(2)}, u32[]{:S(2)}) async-start(f32[4,1,16384]{2,1,0:T(1,128)} %reshape.46), calls=%async_computation.1 | async-start | bytes 524288 | tf_op jit(solution)/shard_map/all_to_all | solution.py:111
  152.7 0.5 broadcast.92
  153.3 1.4 reduce
  154.6 0.7 reshape.45
  155.3 0.6 copy.27
  155.9 0.5 fusion.32
  156.5 0.5 fusion.34
  157.0 1.0 all-to-all-done.1
  158.1 1.4 reduce.1
  159.4 0.7 reshape.47
  160.1 0.6 copy.29
  160.7 0.5 clamp_subtract_fusion.2
  161.3 0.5 clamp_subtract_fusion.3
  161.8 0.5 fusion.65
  163.3 0.5 fusion.18
  164.0 9.7 %all_to_all.96 = f32[64,16,128]{2,1,0:T(8,128)S(1)} all-to-all(f32[64,16,128]{2,1,0:T(8,128)S(1)} %pad_maximum_fusion), channel_id=1, replica_groups=mesh['af'=4,'sa_0'=8,'sa_1'=4,'sa_2'=2] {'af'}, dimensions={0} | all-to-all | bytes 1048576 | tf_op jit(solution)/shard_map/all_to_all | solution.py:29
  173.9 4.7 %fusion.2 = f32[16,16,512]{2,1,0:T(8,128)S(1)} fusion(bf16[32,512,512]{2,1,0:T(8,128)(2,1)} %all-gather.2.cloned.1.call-done, bf16[16,8,512]{2,1,0:T(8,128)(2,1)S(1)} %get-tuple-element.22, bf16[16,8,512]{2,1,0:T(8,128)(2,1)S(1)} %get-tuple-element.21), kind=kOutput, calls=%fused_computation.2 | convolution fusion | flops 134742016 | bytes 9175040 | tf_op jit(solution)/shard_map/frk,fkc->frc/dot_general | solution.py:77
  178.6 4.7 %fusion.10 = f32[16,16,512]{2,1,0:T(8,128)S(1)} fusion(bf16[32,512,512]{2,1,0:T(8,128)(2,1)} %all-gather.2.cloned.1.call-done, bf16[16,8,512]{2,1,0:T(8,128)(2,1)S(1)} %get-tuple-element.22, bf16[16,8,512]{2,1,0:T(8,128)(2,1)S(1)} %get-tuple-element.21), kind=kOutput, calls=%fused_computation.10 | convolution fusion | flops 134742016 | bytes 9175040 | tf_op jit(solution)/shard_map/frk,fkc->frc/dot_general | solution.py:74
  183.3 0.9 multiply_reduce_fusion.1
  184.3 2.3 fusion
  186.6 2.3 fusion.8
  189.1 0.8 copy.31
  190.0 1.5 reshape.48
  191.4 3.4 %all-to-all-start.3 = ((f32[4,1,16384]{2,1,0:T(1,128)}), f32[4,1,16384]{2,1,0:T(1,128)S(1)}, u32[]{:S(2)}, u32[]{:S(2)}) async-start(f32[4,1,16384]{2,1,0:T(1,128)} %reshape.48), calls=%async_computation.3 | async-start | bytes 524288 | tf_op jit(solution)/shard_map/all_to_all | solution.py:110
  194.8 0.8 copy.33
  195.7 1.5 reshape.50
  197.1 3.2 %all-to-all-done.3 = f32[4,1,16384]{2,1,0:T(1,128)S(1)} async-done(((f32[4,1,16384]{2,1,0:T(1,128)}), f32[4,1,16384]{2,1,0:T(1,128)S(1)}, u32[]{:S(2)}, u32[]{:S(2)}) %all-to-all-start.3) | async-done | bytes 262176 | tf_op jit(solution)/shard_map/all_to_all | solution.py:110
  200.3 3.7 %all-to-all-start.4 = ((f32[4,1,16384]{2,1,0:T(1,128)}), f32[4,1,16384]{2,1,0:T(1,128)S(1)}, u32[]{:S(2)}, u32[]{:S(2)}) async-start(f32[4,1,16384]{2,1,0:T(1,128)} %reshape.50), calls=%async_computation.4 | async-start | bytes 524288 | tf_op jit(solution)/shard_map/all_to_all | solution.py:111
  204.0 1.4 reduce.2
  205.4 0.7 reshape.49
  206.0 0.6 copy.32
  206.6 0.6 fusion.26
  207.2 0.5 fusion.28
  207.7 1.5 all-to-all-done.4
  209.2 1.4 reduce.3
  210.6 0.7 reshape.51
  211.3 0.6 copy.34
  211.9 0.6 clamp_subtract_fusion
  212.4 0.5 clamp_subtract_fusion.1
  213.5 0.5 fusion.62
  214.5 0.5 fusion.16
  215.2 0.8 pad_maximum_fusion.1
  216.0 3.5 %all-to-all-start.5 = ((f32[64,16,128]{2,1,0:T(8,128)}), f32[64,16,128]{2,1,0:T(8,128)S(1)}, u32[]{:S(2)}, u32[]{:S(2)}) async-start(f32[64,16,128]{2,1,0:T(8,128)} %pad_maximum_fusion.1), calls=%async_computation.5 | async-start | bytes 1048576 | tf_op jit(solution)/shard_map/all_to_all | solution.py:29
  222.0 9.3 %psum.28 = f32[2]{0:T(128)S(1)} all-reduce(f32[2]{0:T(128)S(1)} %pad_maximum_fusion.15), channel_id=1, replica_groups=mesh['af'=4,'sa_0'=8,'sa_1'=4,'sa_2'=2] {'af'}, use_global_device_ids=true, to_apply=%region_4.5 | all-reduce | flops 2 | bytes 16 | tf_op jit(solution)/shard_map/psum | solution.py:35
  231.3 12.5 %psum.29 = f32[2]{0:T(128)S(1)} all-reduce(f32[2]{0:T(128)S(1)} %psum.28), channel_id=1, replica_groups=mesh['af'=4,'sa_0'=8,'sa_1'=4,'sa_2'=2] {'sa_0'}, use_global_device_ids=true, to_apply=%region_5.6 | all-reduce | flops 2 | bytes 16 | tf_op jit(solution)/shard_map/psum | solution.py:35
  243.8 7.2 %psum.30 = f32[2]{0:T(128)S(1)} all-reduce(f32[2]{0:T(128)S(1)} %psum.29), channel_id=1, replica_groups=mesh['af'=4,'sa_0'=8,'sa_1'=4,'sa_2'=2] {'sa_1'}, use_global_device_ids=true, to_apply=%region_6.7 | all-reduce | flops 2 | bytes 16 | tf_op jit(solution)/shard_map/psum | solution.py:35
  251.1 15.4 %psum.31 = f32[2]{0:T(128)S(1)} all-reduce(f32[2]{0:T(128)S(1)} %psum.30), channel_id=1, replica_groups=mesh['af'=4,'sa_0'=8,'sa_1'=4,'sa_2'=2] {'sa_2'}, use_global_device_ids=true, to_apply=%region_7.8 | all-reduce | flops 2 | bytes 16 | tf_op jit(solution)/shard_map/psum | solution.py:35
  266.5 0.5 broadcast_multiply_fusion
  267.6 0.8 fusion.158
  (46 shorter events, 3.6 us)
Async XLA Ops:
  7.2 114.0 %all-gather.2.cloned.1.call-start = ((), (), s32[]{:S(2)}) async-start(), calls=%async_computation.6 | async-start | bytes 17039360 | tf_op jit(solution)/shard_map/all_gather | solution.py:19
  10.9 120.3 %copy-start.1 = (f32[16,8,512]{2,1,0:T(8,128)S(1)}, f32[16,8,512]{2,1,0:T(8,128)}, u32[]{:S(2)}) copy-start(f32[16,8,512]{2,1,0:T(8,128)} %param.11) | copy-start | bytes 786436
  10.9 120.3 %copy-start.2 = (f32[16,8,512]{2,1,0:T(8,128)S(1)}, f32[16,8,512]{2,1,0:T(8,128)}, u32[]{:S(2)}) copy-start(f32[16,8,512]{2,1,0:T(8,128)} %param.10) | copy-start | bytes 786436
  10.9 120.3 %copy-start.3 = (bf16[16,8,512]{2,1,0:T(8,128)(2,1)S(1)}, bf16[16,8,512]{2,1,0:T(8,128)(2,1)}, u32[]{:S(2)}) copy-start(bf16[16,8,512]{2,1,0:T(8,128)(2,1)} %param.7) | copy-start | bytes 393220
  10.9 120.3 %copy-start.4 = (bf16[16,8,512]{2,1,0:T(8,128)(2,1)S(1)}, bf16[16,8,512]{2,1,0:T(8,128)(2,1)}, u32[]{:S(2)}) copy-start(bf16[16,8,512]{2,1,0:T(8,128)(2,1)} %param.6) | copy-start | bytes 393220
  10.9 120.3 %copy-start.5 = (f32[16]{0:T(128)S(1)}, f32[16]{0:T(128)}, u32[]{:S(2)}) copy-start(f32[16]{0:T(128)} %param.9) | copy-start | bytes 196
  10.9 120.3 %copy-start.6 = (f32[16]{0:T(128)S(1)}, f32[16]{0:T(128)}, u32[]{:S(2)}) copy-start(f32[16]{0:T(128)} %param.8) | copy-start | bytes 196
  121.1 11.0 %copy-start = (bf16[32,512,512]{2,1,0:T(8,128)(2,1)S(1)}, bf16[32,512,512]{2,1,0:T(8,128)(2,1)}, u32[]{:S(2)}) copy-start(bf16[32,512,512]{2,1,0:T(8,128)(2,1)} %all-gather.2.cloned.1.call-done) | copy-start | bytes 50331652
  139.2 9.9 %all-to-all-start = ((f32[4,1,16384]{2,1,0:T(1,128)}), f32[4,1,16384]{2,1,0:T(1,128)S(1)}, u32[]{:S(2)}, u32[]{:S(2)}) async-start(f32[4,1,16384]{2,1,0:T(1,128)} %reshape.44), calls=%async_computation | async-start | bytes 524288 | tf_op jit(solution)/shard_map/all_to_all | solution.py:110
  149.1 8.9 %all-to-all-start.1 = ((f32[4,1,16384]{2,1,0:T(1,128)}), f32[4,1,16384]{2,1,0:T(1,128)S(1)}, u32[]{:S(2)}, u32[]{:S(2)}) async-start(f32[4,1,16384]{2,1,0:T(1,128)} %reshape.46), calls=%async_computation.1 | async-start | bytes 524288 | tf_op jit(solution)/shard_map/all_to_all | solution.py:111
  160.7 23.6 %slice-start = ((s8[16777216]{0:T(1024)(128)(4,1)}), s8[4194304]{0:T(1024)(128)(4,1)S(1)}, s32[]{:S(2)}) async-start(s8[16777216]{0:T(1024)(128)(4,1)} %bitcast.77), calls=%async_computation.7 | async-start | bytes 8388608
  173.7 10.6 %slice-start.1 = ((s8[16777216]{0:T(1024)(128)(4,1)}), s8[4194304]{0:T(1024)(128)(4,1)S(1)}, s32[]{:S(2)}) async-start(s8[16777216]{0:T(1024)(128)(4,1)} %bitcast.77), calls=%async_computation.8 | async-start | bytes 8388608
  173.9 10.5 %slice-start.2 = ((s8[16777216]{0:T(1024)(128)(4,1)}), s8[4194304]{0:T(1024)(128)(4,1)S(1)}, s32[]{:S(2)}) async-start(s8[16777216]{0:T(1024)(128)(4,1)} %bitcast.77), calls=%async_computation.9 | async-start | bytes 8388608
  178.6 5.7 %slice-start.3 = ((s8[16777216]{0:T(1024)(128)(4,1)}), s8[4194304]{0:T(1024)(128)(4,1)S(1)}, s32[]{:S(2)}) async-start(s8[16777216]{0:T(1024)(128)(4,1)} %bitcast.77), calls=%async_computation.10 | async-start | bytes 8388608
  191.4 8.9 %all-to-all-start.3 = ((f32[4,1,16384]{2,1,0:T(1,128)}), f32[4,1,16384]{2,1,0:T(1,128)S(1)}, u32[]{:S(2)}, u32[]{:S(2)}) async-start(f32[4,1,16384]{2,1,0:T(1,128)} %reshape.48), calls=%async_computation.3 | async-start | bytes 524288 | tf_op jit(solution)/shard_map/all_to_all | solution.py:110
  200.3 8.9 %all-to-all-start.4 = ((f32[4,1,16384]{2,1,0:T(1,128)}), f32[4,1,16384]{2,1,0:T(1,128)S(1)}, u32[]{:S(2)}, u32[]{:S(2)}) async-start(f32[4,1,16384]{2,1,0:T(1,128)} %reshape.50), calls=%async_computation.4 | async-start | bytes 524288 | tf_op jit(solution)/shard_map/all_to_all | solution.py:111
  216.0 51.0 %all-to-all-start.5 = ((f32[64,16,128]{2,1,0:T(8,128)}), f32[64,16,128]{2,1,0:T(8,128)S(1)}, u32[]{:S(2)}, u32[]{:S(2)}) async-start(f32[64,16,128]{2,1,0:T(8,128)} %pad_maximum_fusion.1), calls=%async_computation.5 | async-start | bytes 1048576 | tf_op jit(solution)/shard_map/all_to_all | solution.py:29
Sparse Core Ops, SparseCore 0:
  11.2 109.8 all-gather.1
where the time goes:
time: 276 us; the launch traced here: 275 us
  waiting for transfers between devices  120 us (43%)
  blocking collectives  54.1 us (20%)
  matrix products  37 us (13%)
  starting transfers between devices  18.2 us (7%)
  between operations  17 us (6%)
  local copies, waits for them, and re-layouts  16.5 us (6%)
  other arithmetic  12.8 us (5%)
    all_gather x1, waiting for transfers between devices, side_by_side(): lax.all_gather(both, axis, axis=dim, tiled=True)  110 us
    psum x4, blocking collectives, by_axis(): value = lax.psum(value, axis)  44.4 us
    dot_general x2, matrix products, on_device(): jnp.einsum('frk,fkc->frc', left_rows, whole_real, preferred_element_type=...  10.1 us
    all_to_all x1, blocking collectives, in_one_piece(): lax.all_to_all(both, axis, split_axis=split_dim, concat_axis=concat_dim,...  9.72 us
    dot_general x2, matrix products, on_device(): jnp.einsum('frk,fkc->frc', left_rows, whole_imaginary, preferred_element_...  9.44 us
    unnamed x34, local copies, waits for them, and re-layouts  8.78 us
    dot_general x16, matrix products, highest(): jnp.dot(left, right, precision=lax.Precision.HIGHEST, preferred_element_t...  8.37 us
    all_to_all x2, starting transfers between devices, on_device(): lax.all_to_all(stepped_real, 'af', split_axis=2, concat_axis=0, tiled=True)  7.41 us
  transfers between devices with their start and end apart: 6, of which 5 were waited for; matrix products, arithmetic and copies ran while one was open for 5% of the time, Pallas kernels for 0%

commit v1 on v0

--- a/solution.py
+++ b/solution.py
@@ -12,6 +12,28 @@
 AF_SA = ("af", "sa_0", "sa_1", "sa_2")
 STEP_LENGTH = 0.02
 THRESHOLD = 0.25
+
+
+def split_up(shard, dim, size):
+    before, after = (shard.shape[:dim], shard.shape[dim + 1 :])
+    return jnp.moveaxis(shard.reshape(*before, size, -1, *after), dim, 0)
+
+
+def joined_along(blocks, dim):
+    shape = list(blocks.shape[1:])
+    shape[dim] *= blocks.shape[0]
+    return jnp.moveaxis(blocks, 0, dim).reshape(shape)
+
+
+def exchange_directly(x, axis, split_dim, concat_dim):
+    devices, index = (lax.axis_size(axis), lax.axis_index(axis))
+    parts = split_up(x, split_dim, devices)
+    outs = [parts[index]]
+    for step in range(1, devices):
+        sent = parts[(index + step) % devices]
+        outs.append(lax.ppermute(sent, axis, [(i, (i + step) % devices) for i in range(devices)]))
+    parts = jnp.stack(outs)[(index - jnp.arange(devices)) % devices]
+    return joined_along(parts, concat_dim)
 
 
 def side_by_side(arrays, axis, dim, along):
@@ -107,7 +129,7 @@
         stepped_real = current_real + STEP_LENGTH * gradient_real
         stepped_imaginary = current_imaginary + STEP_LENGTH * gradient_imaginary
         trace_real, trace_imaginary = (
-            lax.all_to_all(stepped_real, "af", split_axis=2, concat_axis=0, tiled=True),
+            exchange_directly(stepped_real, "af", 2, 0),
             lax.all_to_all(stepped_imaginary, "af", split_axis=2, concat_axis=0, tiled=True),
         )
         block_shape = trace_real.shape

time: 276 us -> 264 us (0.957)
  local copies, waits for them, and re-layouts: 16.5 us -> 10.7 us
  other arithmetic: 12.8 us -> 10 us
    all_to_all x2 -> x0, starting transfers between devices: 7.41 us -> none  [on_device(): lax.all_to_all(stepped_real, 'af', split_axis=2, concat_axis=0, tiled=True)]
    all_to_all x2 -> x0, waiting for transfers between devices: 6.86 us -> none  [on_device(): lax.all_to_all(stepped_real, 'af', split_axis=2, concat_axis=0, tiled=True)]
    ppermute x0 -> x6, starting transfers between devices: none -> 5.83 us  [exchange_directly(): lax.ppermute(sent, axis, [(i, (i + step) % devices) for i in range(device...]
    all_to_all x2, waiting for transfers between devices: 2.54 us -> 7.48 us  [on_device(): lax.all_to_all(stepped_imaginary, 'af', split_axis=2, concat_axis=0, tile...]
    unnamed x34 -> x30, local copies, waits for them, and re-layouts: 8.78 us -> 4.54 us
  transfers between devices with their start and end apart: 6 -> 10, of which waited for: 5 -> 3; matrix products, arithmetic and copies ran while one was open for 5% -> 4% of each run, Pallas kernels for 0% -> 0%
where the time goes in v1:
time: 264 us; the launch traced here: 263 us
  waiting for transfers between devices  118 us (45%)
  blocking collectives  53.8 us (20%)
  matrix products  37 us (14%)
  starting transfers between devices  17.1 us (6%)
  between operations  17.1 us (6%)
  local copies, waits for them, and re-layouts  10.7 us (4%)
  other arithmetic  10 us (4%)
    all_gather x1, waiting for transfers between devices, side_by_side(): lax.all_gather(both, axis, axis=dim, tiled=True)  110 us
    psum x4, blocking collectives, by_axis(): value = lax.psum(value, axis)  44.5 us
    dot_general x2, matrix products, on_device(): jnp.einsum('frk,fkc->frc', left_rows, whole_real, preferred_element_type=...  10.1 us
    dot_general x2, matrix products, on_device(): jnp.einsum('frk,fkc->frc', left_rows, whole_imaginary, preferred_element_...  9.44 us
    all_to_all x1, blocking collectives, in_one_piece(): lax.all_to_all(both, axis, split_axis=split_dim, concat_axis=concat_dim,...  9.33 us
    dot_general x16, matrix products, highest(): jnp.dot(left, right, precision=lax.Precision.HIGHEST, preferred_element_t...  8.32 us
    all_to_all x2, starting transfers between devices, on_device(): lax.all_to_all(stepped_imaginary, 'af', split_axis=2, concat_axis=0, tile...  7.8 us
    all_to_all x2, waiting for transfers between devices, on_device(): lax.all_to_all(stepped_imaginary, 'af', split_axis=2, concat_axis=0, tile...  7.48 us
  transfers between devices with their start and end apart: 10, of which 3 were waited for; matrix products, arithmetic and copies ran while one was open for 4% of the time, Pallas kernels for 0%

profile of v1, /device:TPU:1, one launch (start us, length us, event | category | flops | bytes accessed | tf_op | source)
XLA Modules:
  0.0 263.3 jit_solution(12426307141581557128)
XLA Ops:
  7.2 1.7 pad_maximum_fusion.3
  9.0 1.0 convert_element_type.66
  9.9 1.0 convert_element_type.67
  11.0 110.1 %all-gather.2.cloned.1.call-done = bf16[32,512,512]{2,1,0:T(8,128)(2,1)} async-done(((bf16[32,8,512]{2,1,0:T(8,128)(2,1)}), bf16[32,512,512]{2,1,0:T(8,128)(2,1)}) %all-gather.2.cloned.1.call-update) | async-done | bytes 16777232 | tf_op jit(solution)/shard_map/all_gather | solution.py:41
  121.1 4.7 %fusion.6 = f32[16,16,512]{2,1,0:T(8,128)S(1)} fusion(bf16[32,512,512]{2,1,0:T(8,128)(2,1)} %all-gather.2.cloned.1.call-done, bf16[16,8,512]{2,1,0:T(8,128)(2,1)S(1)} %convert_element_type.67, bf16[16,8,512]{2,1,0:T(8,128)(2,1)S(1)} %convert_element_type.66), kind=kOutput, calls=%fused_computation.8 | convolution fusion | flops 134742016 | bytes 9175040 | tf_op jit(solution)/shard_map/frk,fkc->frc/dot_general | solution.py:99
  125.9 5.3 %fusion.14 = f32[16,16,512]{2,1,0:T(8,128)S(1)} fusion(bf16[32,512,512]{2,1,0:T(8,128)(2,1)} %all-gather.2.cloned.1.call-done, bf16[16,8,512]{2,1,0:T(8,128)(2,1)S(1)} %convert_element_type.67, bf16[16,8,512]{2,1,0:T(8,128)(2,1)S(1)} %convert_element_type.66), kind=kOutput, calls=%fused_computation.16 | convolution fusion | flops 134742016 | bytes 9175040 | tf_op jit(solution)/shard_map/frk,fkc->frc/dot_general | solution.py:96
  131.2 0.8 multiply_reduce_fusion.3
  132.1 2.3 fusion.4
  134.4 2.3 fusion.12
  136.7 0.2 fusion.45
  137.0 2.5 collective-permute-start.2
  139.5 0.5 collective-permute-start.1
  140.1 0.6 collective-permute-start
  140.7 0.8 copy.20
  141.5 1.5 reshape.121
  142.9 3.6 %all-to-all-start = ((f32[4,1,16384]{2,1,0:T(1,128)}), f32[4,1,16384]{2,1,0:T(1,128)S(1)}, u32[]{:S(2)}, u32[]{:S(2)}) async-start(f32[4,1,16384]{2,1,0:T(1,128)} %reshape.121), calls=%async_computation | async-start | bytes 524288 | tf_op jit(solution)/shard_map/all_to_all | solution.py:133
  146.6 0.6 gather_fusion
  147.2 0.5 fusion.32
  147.7 0.5 fusion.34
  148.2 3.6 %all-to-all-done = f32[4,1,16384]{2,1,0:T(1,128)S(1)} async-done(((f32[4,1,16384]{2,1,0:T(1,128)}), f32[4,1,16384]{2,1,0:T(1,128)S(1)}, u32[]{:S(2)}, u32[]{:S(2)}) %all-to-all-start) | async-done | bytes 262176 | tf_op jit(solution)/shard_map/all_to_all | solution.py:133
  151.8 0.6 broadcast.167
  152.4 1.3 reduce
  153.8 0.7 reshape.122
  154.4 0.6 copy.21
  155.1 0.5 clamp_subtract_fusion.2
  155.6 0.5 clamp_subtract_fusion.3
  156.1 0.5 fusion.67
  156.7 0.5 fusion.66
  157.2 0.5 fusion.19
  157.7 0.5 fusion.18
  158.4 9.3 %all_to_all.66 = f32[64,16,128]{2,1,0:T(8,128)S(1)} all-to-all(f32[64,16,128]{2,1,0:T(8,128)S(1)} %pad_maximum_fusion), channel_id=1, replica_groups=mesh['af'=4,'sa_0'=8,'sa_1'=4,'sa_2'=2] {'af'}, dimensions={0} | all-to-all | bytes 1048576 | tf_op jit(solution)/shard_map/all_to_all | solution.py:51
  167.8 4.7 %fusion.2 = f32[16,16,512]{2,1,0:T(8,128)S(1)} fusion(bf16[32,512,512]{2,1,0:T(8,128)(2,1)} %all-gather.2.cloned.1.call-done, bf16[16,8,512]{2,1,0:T(8,128)(2,1)S(1)} %get-tuple-element.22, bf16[16,8,512]{2,1,0:T(8,128)(2,1)S(1)} %get-tuple-element.21), kind=kOutput, calls=%fused_computation.4 | convolution fusion | flops 134742016 | bytes 9175040 | tf_op jit(solution)/shard_map/frk,fkc->frc/dot_general | solution.py:99
  172.6 4.7 %fusion.10 = f32[16,16,512]{2,1,0:T(8,128)S(1)} fusion(bf16[32,512,512]{2,1,0:T(8,128)(2,1)} %all-gather.2.cloned.1.call-done, bf16[16,8,512]{2,1,0:T(8,128)(2,1)S(1)} %get-tuple-element.22, bf16[16,8,512]{2,1,0:T(8,128)(2,1)S(1)} %get-tuple-element.21), kind=kOutput, calls=%fused_computation.12 | convolution fusion | flops 134742016 | bytes 9175040 | tf_op jit(solution)/shard_map/frk,fkc->frc/dot_general | solution.py:96
  177.3 0.8 multiply_reduce_fusion.1
  178.2 2.3 fusion
  180.5 2.3 fusion.8
  183.1 1.0 collective-permute-start.5
  184.1 1.2 collective-permute-start.4
  185.2 0.8 copy.23
  186.1 1.5 reshape.123
  187.5 4.2 %all-to-all-start.2 = ((f32[4,1,16384]{2,1,0:T(1,128)}), f32[4,1,16384]{2,1,0:T(1,128)S(1)}, u32[]{:S(2)}, u32[]{:S(2)}) async-start(f32[4,1,16384]{2,1,0:T(1,128)} %reshape.123), calls=%async_computation.2 | async-start | bytes 524288 | tf_op jit(solution)/shard_map/all_to_all | solution.py:133
  191.8 0.6 gather_fusion.1
  192.4 0.5 fusion.26
  192.9 0.5 fusion.28
  193.4 3.9 %all-to-all-done.2 = f32[4,1,16384]{2,1,0:T(1,128)S(1)} async-done(((f32[4,1,16384]{2,1,0:T(1,128)}), f32[4,1,16384]{2,1,0:T(1,128)S(1)}, u32[]{:S(2)}, u32[]{:S(2)}) %all-to-all-start.2) | async-done | bytes 262176 | tf_op jit(solution)/shard_map/all_to_all | solution.py:133
  197.3 1.3 reduce.1
  198.6 0.7 reshape.124
  199.3 0.6 copy.24
  199.9 0.6 clamp_subtract_fusion
  200.5 0.5 clamp_subtract_fusion.1
  201.0 0.5 fusion.65
  201.6 0.5 fusion.64
  202.1 0.5 fusion.17
  202.6 0.5 fusion.16
  203.2 0.8 pad_maximum_fusion.1
  204.1 3.5 %all-to-all-start.3 = ((f32[64,16,128]{2,1,0:T(8,128)}), f32[64,16,128]{2,1,0:T(8,128)S(1)}, u32[]{:S(2)}, u32[]{:S(2)}) async-start(f32[64,16,128]{2,1,0:T(8,128)} %pad_maximum_fusion.1), calls=%async_computation.3 | async-start | bytes 1048576 | tf_op jit(solution)/shard_map/all_to_all | solution.py:51
  210.1 9.3 %psum.28 = f32[2]{0:T(128)S(1)} all-reduce(f32[2]{0:T(128)S(1)} %pad_maximum_fusion.17), channel_id=1, replica_groups=mesh['af'=4,'sa_0'=8,'sa_1'=4,'sa_2'=2] {'af'}, use_global_device_ids=true, to_apply=%region_4.5 | all-reduce | flops 2 | bytes 16 | tf_op jit(solution)/shard_map/psum | solution.py:57
  219.3 12.5 %psum.29 = f32[2]{0:T(128)S(1)} all-reduce(f32[2]{0:T(128)S(1)} %psum.28), channel_id=1, replica_groups=mesh['af'=4,'sa_0'=8,'sa_1'=4,'sa_2'=2] {'sa_0'}, use_global_device_ids=true, to_apply=%region_5.6 | all-reduce | flops 2 | bytes 16 | tf_op jit(solution)/shard_map/psum | solution.py:57
  231.8 7.2 %psum.30 = f32[2]{0:T(128)S(1)} all-reduce(f32[2]{0:T(128)S(1)} %psum.29), channel_id=1, replica_groups=mesh['af'=4,'sa_0'=8,'sa_1'=4,'sa_2'=2] {'sa_1'}, use_global_device_ids=true, to_apply=%region_6.7 | all-reduce | flops 2 | bytes 16 | tf_op jit(solution)/shard_map/psum | solution.py:57
  239.1 15.5 %psum.31 = f32[2]{0:T(128)S(1)} all-reduce(f32[2]{0:T(128)S(1)} %psum.30), channel_id=1, replica_groups=mesh['af'=4,'sa_0'=8,'sa_1'=4,'sa_2'=2] {'sa_2'}, use_global_device_ids=true, to_apply=%region_7.8 | all-reduce | flops 2 | bytes 16 | tf_op jit(solution)/shard_map/psum | solution.py:57
  254.5 0.5 broadcast_multiply_fusion
  255.1 0.3 copy.70
  255.4 0.2 all_to_all.61
  255.6 0.8 fusion.162
  (52 shorter events, 1.0 us)
Async XLA Ops:
  7.2 114.0 %all-gather.2.cloned.1.call-start = ((), (), s32[]{:S(2)}) async-start(), calls=%async_computation.4 | async-start | bytes 17039360 | tf_op jit(solution)/shard_map/all_gather | solution.py:41
  11.0 120.2 %copy-start.1 = (f32[16,8,512]{2,1,0:T(8,128)S(1)}, f32[16,8,512]{2,1,0:T(8,128)}, u32[]{:S(2)}) copy-start(f32[16,8,512]{2,1,0:T(8,128)} %param.11) | copy-start | bytes 786436
  11.0 120.2 %copy-start.2 = (f32[16,8,512]{2,1,0:T(8,128)S(1)}, f32[16,8,512]{2,1,0:T(8,128)}, u32[]{:S(2)}) copy-start(f32[16,8,512]{2,1,0:T(8,128)} %param.10) | copy-start | bytes 786436
  11.0 120.2 %copy-start.3 = (bf16[16,8,512]{2,1,0:T(8,128)(2,1)S(1)}, bf16[16,8,512]{2,1,0:T(8,128)(2,1)}, u32[]{:S(2)}) copy-start(bf16[16,8,512]{2,1,0:T(8,128)(2,1)} %param.7) | copy-start | bytes 393220
  11.0 120.2 %copy-start.4 = (bf16[16,8,512]{2,1,0:T(8,128)(2,1)S(1)}, bf16[16,8,512]{2,1,0:T(8,128)(2,1)}, u32[]{:S(2)}) copy-start(bf16[16,8,512]{2,1,0:T(8,128)(2,1)} %param.6) | copy-start | bytes 393220
  11.0 120.2 %copy-start.5 = (f32[16]{0:T(128)S(1)}, f32[16]{0:T(128)}, u32[]{:S(2)}) copy-start(f32[16]{0:T(128)} %param.9) | copy-start | bytes 196
  11.0 120.2 %copy-start.6 = (f32[16]{0:T(128)S(1)}, f32[16]{0:T(128)}, u32[]{:S(2)}) copy-start(f32[16]{0:T(128)} %param.8) | copy-start | bytes 196
  121.1 11.0 %copy-start = (bf16[32,512,512]{2,1,0:T(8,128)(2,1)S(1)}, bf16[32,512,512]{2,1,0:T(8,128)(2,1)}, u32[]{:S(2)}) copy-start(bf16[32,512,512]{2,1,0:T(8,128)(2,1)} %all-gather.2.cloned.1.call-done) | copy-start | bytes 50331652
  137.0 9.6 %collective-permute-start.2 = (f32[16,8,128]{2,1,0:T(8,128)S(1)}, f32[16,8,128]{2,1,0:T(8,128)S(1)}, u32[]{:S(2)}, u32[]{:S(2)}) collective-permute-start(f32[16,8,128]{2,1,0:T(8,128)S(1)} %get-tuple-element.28), channel_id=1, source_target_pairs={{0,192},{64,0},{128,64},{192,128},{1,193},{65,1},{129,65},{193,129... | collective-permute-start | bytes 196616 | tf_op jit(solution)/shard_map/ppermute | solution.py:34
  139.5 7.0 %collective-permute-start.1 = (f32[16,8,128]{2,1,0:T(8,128)S(1)}, f32[16,8,128]{2,1,0:T(8,128)S(1)}, u32[]{:S(2)}, u32[]{:S(2)}) collective-permute-start(f32[16,8,128]{2,1,0:T(8,128)S(1)} %get-tuple-element.29), channel_id=1, source_target_pairs={{0,128},{64,192},{128,0},{192,64},{1,129},{65,193},{129,1},{193,65... | collective-permute-start | bytes 196616 | tf_op jit(solution)/shard_map/ppermute | solution.py:34
  140.1 6.5 %collective-permute-start = (f32[16,8,128]{2,1,0:T(8,128)S(1)}, f32[16,8,128]{2,1,0:T(8,128)S(1)}, u32[]{:S(2)}, u32[]{:S(2)}) collective-permute-start(f32[16,8,128]{2,1,0:T(8,128)S(1)} %get-tuple-element.30), channel_id=1, source_target_pairs={{0,64},{64,128},{128,192},{192,0},{1,65},{65,129},{129,193},{193,1... | collective-permute-start | bytes 196616 | tf_op jit(solution)/shard_map/ppermute | solution.py:34
  142.9 8.9 %all-to-all-start = ((f32[4,1,16384]{2,1,0:T(1,128)}), f32[4,1,16384]{2,1,0:T(1,128)S(1)}, u32[]{:S(2)}, u32[]{:S(2)}) async-start(f32[4,1,16384]{2,1,0:T(1,128)} %reshape.121), calls=%async_computation | async-start | bytes 524288 | tf_op jit(solution)/shard_map/all_to_all | solution.py:133
  155.1 23.1 %slice-start = ((s8[16777216]{0:T(1024)(128)(4,1)}), s8[4194304]{0:T(1024)(128)(4,1)S(1)}, s32[]{:S(2)}) async-start(s8[16777216]{0:T(1024)(128)(4,1)} %bitcast.97), calls=%async_computation.5 | async-start | bytes 8388608
  167.7 10.5 %slice-start.1 = ((s8[16777216]{0:T(1024)(128)(4,1)}), s8[4194304]{0:T(1024)(128)(4,1)S(1)}, s32[]{:S(2)}) async-start(s8[16777216]{0:T(1024)(128)(4,1)} %bitcast.97), calls=%async_computation.6 | async-start | bytes 8388608
  167.8 10.4 %slice-start.2 = ((s8[16777216]{0:T(1024)(128)(4,1)}), s8[4194304]{0:T(1024)(128)(4,1)S(1)}, s32[]{:S(2)}) async-start(s8[16777216]{0:T(1024)(128)(4,1)} %bitcast.97), calls=%async_computation.7 | async-start | bytes 8388608
  172.6 5.7 %slice-start.3 = ((s8[16777216]{0:T(1024)(128)(4,1)}), s8[4194304]{0:T(1024)(128)(4,1)S(1)}, s32[]{:S(2)}) async-start(s8[16777216]{0:T(1024)(128)(4,1)} %bitcast.97), calls=%async_computation.8 | async-start | bytes 8388608
  183.1 8.7 %collective-permute-start.5 = (f32[16,8,128]{2,1,0:T(8,128)S(1)}, f32[16,8,128]{2,1,0:T(8,128)S(1)}, u32[]{:S(2)}, u32[]{:S(2)}) collective-permute-start(f32[16,8,128]{2,1,0:T(8,128)S(1)} %get-tuple-element.24), channel_id=1, source_target_pairs={{0,192},{64,0},{128,64},{192,128},{1,193},{65,1},{129,65},{193,129... | collective-permute-start | bytes 196616 | tf_op jit(solution)/shard_map/ppermute | solution.py:34
  184.1 7.7 %collective-permute-start.4 = (f32[16,8,128]{2,1,0:T(8,128)S(1)}, f32[16,8,128]{2,1,0:T(8,128)S(1)}, u32[]{:S(2)}, u32[]{:S(2)}) collective-permute-start(f32[16,8,128]{2,1,0:T(8,128)S(1)} %get-tuple-element.25), channel_id=1, source_target_pairs={{0,128},{64,192},{128,0},{192,64},{1,129},{65,193},{129,1},{193,65... | collective-permute-start | bytes 196616 | tf_op jit(solution)/shard_map/ppermute | solution.py:34
  185.2 6.5 %collective-permute-start.3 = (f32[16,8,128]{2,1,0:T(8,128)S(1)}, f32[16,8,128]{2,1,0:T(8,128)S(1)}, u32[]{:S(2)}, u32[]{:S(2)}) collective-permute-start(f32[16,8,128]{2,1,0:T(8,128)S(1)} %get-tuple-element.26), channel_id=1, source_target_pairs={{0,64},{64,128},{128,192},{192,0},{1,65},{65,129},{129,193},{193,1... | collective-permute-start | bytes 196616 | tf_op jit(solution)/shard_map/ppermute | solution.py:34
  187.5 9.7 %all-to-all-start.2 = ((f32[4,1,16384]{2,1,0:T(1,128)}), f32[4,1,16384]{2,1,0:T(1,128)S(1)}, u32[]{:S(2)}, u32[]{:S(2)}) async-start(f32[4,1,16384]{2,1,0:T(1,128)} %reshape.123), calls=%async_computation.2 | async-start | bytes 524288 | tf_op jit(solution)/shard_map/all_to_all | solution.py:133
  204.1 51.0 %all-to-all-start.3 = ((f32[64,16,128]{2,1,0:T(8,128)}), f32[64,16,128]{2,1,0:T(8,128)S(1)}, u32[]{:S(2)}, u32[]{:S(2)}) async-start(f32[64,16,128]{2,1,0:T(8,128)} %pad_maximum_fusion.1), calls=%async_computation.3 | async-start | bytes 1048576 | tf_op jit(solution)/shard_map/all_to_all | solution.py:51
Sparse Core Ops, SparseCore 0:
  11.2 109.8 all-gather.1
